TPU v7x, 128 devices: a whole 4x4x4 slice. The times are simulated.
128 devices in a mesh: layer: 2 (over core), px: 16 (over x, z), py: 4 (over y).
Axes of the slice: x: 4, y: 4, z: 4, core: 2. Of those that a mesh axis runs over, the one named last changes fastest.
Arguments:
- right_side: float32 [8, 2048, 4096], P('layer', 'px', 'py'), may hold values from -30 to 30
- row_conduct: float32 [8, 2048, 4096], P('layer', 'px', 'py'), may hold values from 0.5 to 2
- column_conduct: float32 [8, 2048, 4096], P('layer', 'px', 'py'), may hold values from 0.5 to 2
- via_conduct: float32 [8, 2048, 4096], P('layer', 'px', 'py'), may hold values from 0.5 to 4
- via_mask: int32 [8, 2048, 4096], P('layer', 'px', 'py'), may hold values 0 or 1
- ground_conduct: float32 [8, 2048, 4096], P('layer', 'px', 'py'), may hold values from 0.01 to 0.1
Outputs:
- solution_field: float32 [8, 2048, 4096], P('layer', 'px', 'py')
- residual: float32 [8, 2048, 4096], P('layer', 'px', 'py')
All inputs are finite; a program needn't handle non-finite values. No bound on the sum of `via_mask` on one device may be relied on, other than what follows from the above.
Results may differ from a plain program's by a relative error of at most 0.0001.
Values sent between devices are 32-bit elements; how exact they have to be, the bound alone decides.
A program may use at most 128 MiB of HBM per device.

v0:
```python
import jax
import jax.numpy as jnp
from jax import lax
from jax.sharding import Mesh
from jax.sharding import PartitionSpec as P

ITERS = 2
LAYER_PX_PY = ("layer", "px_0", "px_1", "py")
PX = ("px_0", "px_1")


def extended(value, sides, width):
    edges = {}
    for axis, dim in sides:
        count, length = (lax.axis_size(axis), value.shape[dim])
        up = [(i, (i + 1) % count) for i in range(count - 1)]
        last = lax.slice_in_dim(value, length - width, length, axis=dim)
        initial = lax.slice_in_dim(value, 0, width, axis=dim)
        edges[dim] = (
            lax.ppermute(last, axis, up),
            lax.ppermute(initial, axis, [(b, a) for a, b in up]),
        )
    done = []
    for _, dim in sides:
        low, high = edges[dim]
        around = [(width, width) if d in done else (0, 0) for d in range(value.ndim)]
        value = jnp.concatenate([jnp.pad(low, around), value, jnp.pad(high, around)], axis=dim)
        done.append(dim)
    return value


def by_axis(value, axes):
    for axis in axes:
        value = lax.psum(value, axis)
    return value


def from_behind(value, axis, by):
    count = lax.axis_size(axis)
    pairs = [(i, i + by) for i in range(count) if 0 <= i + by < count]
    return lax.ppermute(value, axis, pairs)


def factor_layers(diagonal, vertical, vertical_below, carried):
    gains = []
    inverses = []
    previous = carried
    for index in range(diagonal.shape[0]):
        inverse = 1.0 / (diagonal[index] - vertical_below[index] * previous)
        previous = vertical[index] * inverse
        gains.append(previous)
        inverses.append(inverse)
    return (jnp.stack(gains), jnp.stack(inverses))


def forward_layers(residual, vertical_below, inverses, carried):
    values = []
    previous = carried
    for index in range(residual.shape[0]):
        previous = (residual[index] + vertical_below[index] * previous) * inverses[index]
        values.append(previous)
    return jnp.stack(values)


def back_layers(forward, gains, carried):
    count = forward.shape[0]
    values = [None] * count
    following = carried
    for index in range(count - 1, -1, -1):
        following = forward[index] + gains[index] * following
        values[index] = following
    return jnp.stack(values)


def operate(field, coeffs):
    diagonal, row_conduct, row_upper, column_conduct, column_left, vertical, vertical_below = coeffs
    padded = extended(field, (("layer", 0), (PX, 1), ("py", 2)), 1)
    return (
        diagonal * field
        - row_conduct * padded[1:-1, 2:, 1:-1]
        - row_upper * padded[1:-1, :-2, 1:-1]
        - column_conduct * padded[1:-1, 1:-1, 2:]
        - column_left * padded[1:-1, 1:-1, :-2]
        - vertical * padded[2:, 1:-1, 1:-1]
        - vertical_below * padded[:-2, 1:-1, 1:-1]
    )


def paired_sums(residual, precond, image):
    return (
        by_axis(jnp.sum(residual * precond), LAYER_PX_PY),
        by_axis(jnp.sum(image * precond), LAYER_PX_PY),
    )


def shards(right_side, row_conduct, column_conduct, via_conduct, via_mask, ground_conduct):
    depth = right_side.shape[0]
    members = lax.axis_size("layer")
    layers_total = depth * members
    level = lax.axis_index("layer") * depth + jnp.arange(depth, dtype=jnp.int32)
    keep = (level < layers_total - 1).astype(jnp.float32)[:, None, None]
    vertical = via_conduct * via_mask.astype(jnp.float32) * keep
    row_edge = from_behind(row_conduct[:, -1:, :], PX, 1)
    row_upper = jnp.concatenate([row_edge, row_conduct[:, :-1, :]], axis=1)
    column_edge = from_behind(column_conduct[:, :, -1:], "py", 1)
    column_left = jnp.concatenate([column_edge, column_conduct[:, :, :-1]], axis=2)
    vertical_edge = from_behind(vertical[-1:], "layer", 1)
    vertical_below = jnp.concatenate([vertical_edge, vertical[:-1]], axis=0)
    diagonal = (
        ground_conduct
        + row_conduct
        + row_upper
        + column_conduct
        + column_left
        + vertical
        + vertical_below
    )
    coeffs = (
        diagonal,
        row_conduct,
        row_upper,
        column_conduct,
        column_left,
        vertical,
        vertical_below,
    )
    plane = jnp.zeros_like(right_side[0])
    carried = plane
    gains, inverses = factor_layers(diagonal, vertical, vertical_below, carried)
    carried = from_behind(gains[-1], "layer", 1)
    gains, inverses = factor_layers(diagonal, vertical, vertical_below, carried)

    def precondition(residual):
        incoming = plane
        forward = forward_layers(residual, vertical_below, inverses, incoming)
        incoming = from_behind(forward[-1], "layer", 1)
        forward = forward_layers(residual, vertical_below, inverses, incoming)
        returning = plane
        solved = back_layers(forward, gains, returning)
        returning = from_behind(solved[0], "layer", -1)
        return back_layers(forward, gains, returning)

    solution_field = jnp.zeros_like(right_side)
    residual = right_side
    precond = precondition(residual)
    image = operate(precond, coeffs)
    rho, curvature = paired_sums(residual, precond, image)
    alpha = rho / curvature
    direction, along = (precond, image)
    for step in range(ITERS):
        solution_field = solution_field + alpha * direction
        residual = residual - alpha * along
        if step + 1 < ITERS:
            precond = precondition(residual)
            image = operate(precond, coeffs)
            rho_next, curvature = paired_sums(residual, precond, image)
            ratio = rho_next / rho
            alpha = rho_next / (curvature - ratio * rho_next / alpha)
            direction = precond + ratio * direction
            along = image + ratio * along
            rho = rho_next
    return (solution_field, residual)


def solution(mesh):
    split = Mesh(
        mesh.devices.reshape(mesh.shape["layer"], 4, 4, mesh.shape["py"]),
        ("layer", "px_0", "px_1", "py"),
    )
    return jax.shard_map(
        shards,
        mesh=split,
        in_specs=(
            P("layer", PX, "py"),
            P("layer", PX, "py"),
            P("layer", PX, "py"),
            P("layer", PX, "py"),
            P("layer", PX, "py"),
            P("layer", PX, "py"),
        ),
        out_specs=(P("layer", PX, "py"), P("layer", PX, "py")),
        check_vma=False,
    )
```

profile of v0, /device:TPU:2, one launch (start us, length us, event | category | flops | bytes accessed | tf_op | source)
XLA Modules:
  0.0 200.5 jit_solution(8595721129554607159)
XLA Ops:
  0.7 2.9 %multiply_multiply_fusion = f32[4,128,1024]{2,1,0:T(8,128)S(1)} fusion(f32[4,128,1024]{2,1,0:T(8,128)} %param.9, s32[4,128,1024]{2,1,0:T(8,128)} %param.10, f32[4]{0:T(128)S(1)} %compare_convert_fusion), kind=kLoop, calls=%fused_computation.59 | loop fusion | flops 1572864 | bytes 6291472 | tf_op jit(solution)/shard_map/mul | solution.py:102
  3.7 1.9 collective-permute-start
  5.6 3.8 %collective-permute-start.1 = (f32[4,1,1024]{2,1,0:T(1,128)S(1)}, f32[4,1,1024]{2,1,0:T(1,128)S(1)}, u32[]{:S(2)}, u32[]{:S(2)}) collective-permute-start(f32[4,1,1024]{2,1,0:T(1,128)S(1)} %slice.173), channel_id=1, source_target_pairs={{0,4},{4,8},{8,12},{12,16},{16,20},{20,24},{24,28},{28,32},{32,36}... | collective-permute-start | bytes 49160 | tf_op jit(solution)/shard_map/ppermute | solution.py:41
  9.6 3.5 %collective-permute-start.2 = (f32[4,128,1]{2,1,0:T(8,128)S(1)}, f32[4,128,1]{2,1,0:T(8,128)S(1)}, u32[]{:S(2)}, u32[]{:S(2)}) collective-permute-start(f32[4,128,1]{2,1,0:T(8,128)S(1)} %slice.175), channel_id=1, source_target_pairs={{0,1},{1,2},{2,3},{4,5},{5,6},{6,7},{8,9},{9,10},{10,11},{12,13},{... | collective-permute-start | bytes 6152 | tf_op jit(solution)/shard_map/ppermute | solution.py:41
  13.2 4.7 %collective-permute-done.2 = f32[4,128,1]{2,1,0:T(8,128)S(1)} collective-permute-done((f32[4,128,1]{2,1,0:T(8,128)S(1)}, f32[4,128,1]{2,1,0:T(8,128)S(1)}, u32[]{:S(2)}, u32[]{:S(2)}) %collective-permute-start.2) | collective-permute-done | bytes 2080 | tf_op jit(solution)/shard_map/ppermute | solution.py:41
  17.9 1.8 add_add_fusion
  24.1 2.3 %collective-permute-start.4 = (f32[128,1024]{1,0:T(8,128)S(1)}, f32[128,1024]{1,0:T(8,128)S(1)}, u32[]{:S(2)}, u32[]{:S(2)}) collective-permute-start(f32[128,1024]{1,0:T(8,128)S(1)} %get-tuple-element.40), channel_id=1, source_target_pairs={{0,64},{1,65},{2,66},{3,67},{4,68},{5,69},{6,70},{7,71},{8,72},{9,... | collective-permute-start | bytes 1572872 | tf_op jit(solution)/shard_map/ppermute | solution.py:41
  30.2 2.5 %collective-permute-done.5 = f32[128,1024]{1,0:T(8,128)S(1)} collective-permute-done((f32[128,1024]{1,0:T(8,128)S(1)}, f32[128,1024]{1,0:T(8,128)S(1)}, u32[]{:S(2)}, u32[]{:S(2)}) %collective-permute-start.5) | collective-permute-done | bytes 524320 | tf_op jit(solution)/shard_map/ppermute | solution.py:41
  33.0 2.1 %collective-permute-start.6 = (f32[1,128,1024]{2,1,0:T(8,128)S(1)}, f32[1,128,1024]{2,1,0:T(8,128)S(1)}, u32[]{:S(2)}, u32[]{:S(2)}) collective-permute-start(f32[1,128,1024]{2,1,0:T(8,128)S(1)} %bitcast.233), channel_id=1, source_target_pairs={{0,64},{1,65},{2,66},{3,67},{4,68},{5,69},{6,70},{7,71},{8,72},{9,... | collective-permute-start | bytes 1572872 | tf_op jit(solution)/shard_map/ppermute | solution.py:20
  39.1 4.0 %collective-permute-start.9 = (f32[4,1,1024]{2,1,0:T(1,128)S(1)}, f32[4,1,1024]{2,1,0:T(1,128)S(1)}, u32[]{:S(2)}, u32[]{:S(2)}) collective-permute-start(f32[4,1,1024]{2,1,0:T(1,128)S(1)} %get-tuple-element.54), channel_id=1, source_target_pairs={{0,4},{4,8},{8,12},{12,16},{16,20},{20,24},{24,28},{28,32},{32,36}... | collective-permute-start | bytes 49160 | tf_op jit(solution)/shard_map/ppermute | solution.py:20
  43.0 4.1 %collective-permute-start.8 = (f32[4,1,1024]{2,1,0:T(1,128)S(1)}, f32[4,1,1024]{2,1,0:T(1,128)S(1)}, u32[]{:S(2)}, u32[]{:S(2)}) collective-permute-start(f32[4,1,1024]{2,1,0:T(1,128)S(1)} %get-tuple-element.55), channel_id=1, source_target_pairs={{4,0},{8,4},{12,8},{16,12},{20,16},{24,20},{28,24},{32,28},{36,32}... | collective-permute-start | bytes 49160 | tf_op jit(solution)/shard_map/ppermute | solution.py:21
  48.6 5.0 %collective-permute-start.11 = (f32[4,128,1]{2,1,0:T(8,128)S(1)}, f32[4,128,1]{2,1,0:T(8,128)S(1)}, u32[]{:S(2)}, u32[]{:S(2)}) collective-permute-start(f32[4,128,1]{2,1,0:T(8,128)S(1)} %get-tuple-element.53), channel_id=1, source_target_pairs={{0,1},{1,2},{2,3},{4,5},{5,6},{6,7},{8,9},{9,10},{10,11},{12,13},{... | collective-permute-start | bytes 6152 | tf_op jit(solution)/shard_map/ppermute | solution.py:20
  54.6 4.2 %collective-permute-done.10 = f32[4,128,1]{2,1,0:T(8,128)S(1)} collective-permute-done((f32[4,128,1]{2,1,0:T(8,128)S(1)}, f32[4,128,1]{2,1,0:T(8,128)S(1)}, u32[]{:S(2)}, u32[]{:S(2)}) %collective-permute-start.10) | collective-permute-done | bytes 2080 | tf_op jit(solution)/shard_map/ppermute | solution.py:21
  60.0 9.9 %multiply_reduce_fusion.2 = (f32[]{:T(128)}, f32[]{:T(128)}, f32[4,128,1024]{2,1,0:T(8,128)}) fusion(f32[1,128,1024]{2,1,0:T(8,128)S(1)} %bitcast.235, f32[1,128,1024]{2,1,0:T(8,128)S(1)} %bitcast.245, f32[1,128,1024]{2,1,0:T(8,128)S(1)} %bitcast.242, f32[1,128,1024]{2,1,0:T(8,128)S(1)} %get-tuple-element.33, f32[4,128,1024]{2,1,0:T(8,128)S(1)} %copy-done.5, ...), kind=kLoop, calls=%fused_computation.56 | loop fusion | flops 25690112 | bytes 25219080 | tf_op jit(solution)/shard_map/reduce_sum | solution.py:92
  69.9 3.1 %all-reduce.15 = (f32[]{:T(128)}, f32[]{:T(128)}) all-reduce(f32[]{:T(128)} %get-tuple-element.5, f32[]{:T(128)} %get-tuple-element.4), channel_id=1, replica_groups=mesh['layer'=2,'px_0'=4,'px_1'=4,'py'=4] {'layer'}, use_global_device_ids=true, to_apply=%region_1.2 | all-reduce | flops 2 | bytes 16 | tf_op jit(solution)/shard_map/psum | solution.py:34
  73.0 9.3 %all-reduce.13 = (f32[]{:T(128)}, f32[]{:T(128)}) all-reduce(f32[]{:T(128)} %get-tuple-element.20, f32[]{:T(128)} %get-tuple-element.21), channel_id=1, replica_groups=mesh['layer'=2,'px_0'=4,'px_1'=4,'py'=4] {'px_0'}, use_global_device_ids=true, to_apply=%region_2.3 | all-reduce | flops 2 | bytes 16 | tf_op jit(solution)/shard_map/psum | solution.py:34
  82.3 8.7 %all-reduce.11 = (f32[]{:T(128)}, f32[]{:T(128)}) all-reduce(f32[]{:T(128)} %get-tuple-element.16, f32[]{:T(128)} %get-tuple-element.17), channel_id=1, replica_groups=mesh['layer'=2,'px_0'=4,'px_1'=4,'py'=4] {'px_1'}, use_global_device_ids=true, to_apply=%region_3.4 | all-reduce | flops 2 | bytes 16 | tf_op jit(solution)/shard_map/psum | solution.py:34
  91.0 12.8 %all-reduce.9 = (f32[]{:T(128)}, f32[]{:T(128)}) all-reduce(f32[]{:T(128)} %get-tuple-element.12, f32[]{:T(128)} %get-tuple-element.13), channel_id=1, replica_groups=mesh['layer'=2,'px_0'=4,'px_1'=4,'py'=4] {'py'}, use_global_device_ids=true, to_apply=%region_4.5 | all-reduce | flops 2 | bytes 16 | tf_op jit(solution)/shard_map/psum | solution.py:34
  105.3 2.8 %multiply_subtract_fusion.1 = f32[4,128,1024]{2,1,0:T(8,128)S(1)} fusion(f32[4,128,1024]{2,1,0:T(8,128)} %param.6, f32[4,128,1024]{2,1,0:T(8,128)} %get-tuple-element.31, f32[]{:T(128)S(6)} %div.44), kind=kLoop, calls=%fused_computation.55 | loop fusion | flops 1048576 | bytes 6291460 | tf_op jit(solution)/shard_map/sub | solution.py:152
  108.8 1.6 collective-permute-start.12
  114.1 2.5 %collective-permute-done.13 = f32[128,1024]{1,0:T(8,128)S(1)} collective-permute-done((f32[128,1024]{1,0:T(8,128)S(1)}, f32[128,1024]{1,0:T(8,128)S(1)}, u32[]{:S(2)}, u32[]{:S(2)}) %collective-permute-start.13) | collective-permute-done | bytes 524320 | tf_op jit(solution)/shard_map/ppermute | solution.py:41
  116.9 2.1 %collective-permute-start.14 = (f32[1,128,1024]{2,1,0:T(8,128)S(1)}, f32[1,128,1024]{2,1,0:T(8,128)S(1)}, u32[]{:S(2)}, u32[]{:S(2)}) collective-permute-start(f32[1,128,1024]{2,1,0:T(8,128)S(1)} %bitcast.237), channel_id=1, source_target_pairs={{0,64},{1,65},{2,66},{3,67},{4,68},{5,69},{6,70},{7,71},{8,72},{9,... | collective-permute-start | bytes 1572872 | tf_op jit(solution)/shard_map/ppermute | solution.py:20
  125.8 3.9 %collective-permute-start.17 = (f32[4,1,1024]{2,1,0:T(1,128)S(1)}, f32[4,1,1024]{2,1,0:T(1,128)S(1)}, u32[]{:S(2)}, u32[]{:S(2)}) collective-permute-start(f32[4,1,1024]{2,1,0:T(1,128)S(1)} %get-tuple-element.50), channel_id=1, source_target_pairs={{0,4},{4,8},{8,12},{12,16},{16,20},{20,24},{24,28},{28,32},{32,36}... | collective-permute-start | bytes 49160 | tf_op jit(solution)/shard_map/ppermute | solution.py:20
  129.7 4.3 %collective-permute-start.16 = (f32[4,1,1024]{2,1,0:T(1,128)S(1)}, f32[4,1,1024]{2,1,0:T(1,128)S(1)}, u32[]{:S(2)}, u32[]{:S(2)}) collective-permute-start(f32[4,1,1024]{2,1,0:T(1,128)S(1)} %get-tuple-element.51), channel_id=1, source_target_pairs={{4,0},{8,4},{12,8},{16,12},{20,16},{24,20},{28,24},{32,28},{36,32}... | collective-permute-start | bytes 49160 | tf_op jit(solution)/shard_map/ppermute | solution.py:21
  136.4 4.6 %collective-permute-start.19 = (f32[4,128,1]{2,1,0:T(8,128)S(1)}, f32[4,128,1]{2,1,0:T(8,128)S(1)}, u32[]{:S(2)}, u32[]{:S(2)}) collective-permute-start(f32[4,128,1]{2,1,0:T(8,128)S(1)} %get-tuple-element.49), channel_id=1, source_target_pairs={{0,1},{1,2},{2,3},{4,5},{5,6},{6,7},{8,9},{9,10},{10,11},{12,13},{... | collective-permute-start | bytes 6152 | tf_op jit(solution)/shard_map/ppermute | solution.py:20
  141.8 3.9 %collective-permute-done.18 = f32[4,128,1]{2,1,0:T(8,128)S(1)} collective-permute-done((f32[4,128,1]{2,1,0:T(8,128)S(1)}, f32[4,128,1]{2,1,0:T(8,128)S(1)}, u32[]{:S(2)}, u32[]{:S(2)}) %collective-permute-start.18) | collective-permute-done | bytes 2080 | tf_op jit(solution)/shard_map/ppermute | solution.py:21
  147.0 10.1 %multiply_reduce_fusion = (f32[]{:T(128)}, f32[]{:T(128)}, f32[4,128,1024]{2,1,0:T(8,128)}) fusion(f32[1,128,1024]{2,1,0:T(8,128)S(1)} %bitcast.239, f32[1,128,1024]{2,1,0:T(8,128)S(1)} %bitcast.251, f32[1,128,1024]{2,1,0:T(8,128)S(1)} %bitcast.248, f32[1,128,1024]{2,1,0:T(8,128)S(1)} %get-tuple-element.24, f32[4,128,1024]{2,1,0:T(8,128)S(1)} %multiply_subtract_fusion.1, ...), kind=kLoop, calls=%fused_computation.53 | loop fusion | flops 25690112 | bytes 25219080 | tf_op jit(solution)/shard_map/reduce_sum | solution.py:92
  157.1 3.1 %all-reduce.14 = (f32[]{:T(128)}, f32[]{:T(128)}) all-reduce(f32[]{:T(128)} %get-tuple-element.3, f32[]{:T(128)} %get-tuple-element.2), channel_id=1, replica_groups=mesh['layer'=2,'px_0'=4,'px_1'=4,'py'=4] {'layer'}, use_global_device_ids=true, to_apply=%region_11.12 | all-reduce | flops 2 | bytes 16 | tf_op jit(solution)/shard_map/psum | solution.py:34
  160.2 9.0 %all-reduce.12 = (f32[]{:T(128)}, f32[]{:T(128)}) all-reduce(f32[]{:T(128)} %get-tuple-element.18, f32[]{:T(128)} %get-tuple-element.19), channel_id=1, replica_groups=mesh['layer'=2,'px_0'=4,'px_1'=4,'py'=4] {'px_0'}, use_global_device_ids=true, to_apply=%region_12.13 | all-reduce | flops 2 | bytes 16 | tf_op jit(solution)/shard_map/psum | solution.py:34
  169.1 9.8 %all-reduce.10 = (f32[]{:T(128)}, f32[]{:T(128)}) all-reduce(f32[]{:T(128)} %get-tuple-element.14, f32[]{:T(128)} %get-tuple-element.15), channel_id=1, replica_groups=mesh['layer'=2,'px_0'=4,'px_1'=4,'py'=4] {'px_1'}, use_global_device_ids=true, to_apply=%region_13.14 | all-reduce | flops 2 | bytes 16 | tf_op jit(solution)/shard_map/psum | solution.py:34
  178.9 10.9 %all-reduce.8 = (f32[]{:T(128)}, f32[]{:T(128)}) all-reduce(f32[]{:T(128)} %get-tuple-element.10, f32[]{:T(128)} %get-tuple-element.11), channel_id=1, replica_groups=mesh['layer'=2,'px_0'=4,'px_1'=4,'py'=4] {'py'}, use_global_device_ids=true, to_apply=%region_14.15 | all-reduce | flops 2 | bytes 16 | tf_op jit(solution)/shard_map/psum | solution.py:34
  194.4 6.0 %multiply_subtract_fusion = (f32[4,128,1024]{2,1,0:T(8,128)}, f32[4,128,1024]{2,1,0:T(8,128)}) fusion(f32[4,128,1024]{2,1,0:T(8,128)} %copy-done.4, f32[4,128,1024]{2,1,0:T(8,128)} %get-tuple-element.22, f32[4,128,1024]{2,1,0:T(8,128)} %get-tuple-element.31, f32[]{:T(128)S(6)} %div.45, f32[]{:T(128)S(6)} %div.47, f32[1,128,1024]{2,1,0:T(8,128)} %bitcast.240, ...), kind=kLoop, calls=%fused_computation.51 | loop fusion | flops 7864320 | bytes 14680076 | tf_op jit(solution)/shard_map/sub | solution.py:152
  (124 shorter events, 31.8 us)
Async XLA Ops:
  3.7 14.2 %collective-permute-start = (f32[1,128,1024]{2,1,0:T(8,128)S(1)}, f32[1,128,1024]{2,1,0:T(8,128)S(1)}, u32[]{:S(2)}, u32[]{:S(2)}) collective-permute-start(f32[1,128,1024]{2,1,0:T(8,128)S(1)} %slice.202), channel_id=1, source_target_pairs={{0,64},{1,65},{2,66},{3,67},{4,68},{5,69},{6,70},{7,71},{8,72},{9,... | collective-permute-start | bytes 1572872 | tf_op jit(solution)/shard_map/ppermute | solution.py:41
  5.6 12.3 %collective-permute-start.1 = (f32[4,1,1024]{2,1,0:T(1,128)S(1)}, f32[4,1,1024]{2,1,0:T(1,128)S(1)}, u32[]{:S(2)}, u32[]{:S(2)}) collective-permute-start(f32[4,1,1024]{2,1,0:T(1,128)S(1)} %slice.173), channel_id=1, source_target_pairs={{0,4},{4,8},{8,12},{12,16},{16,20},{20,24},{24,28},{28,32},{32,36}... | collective-permute-start | bytes 49160 | tf_op jit(solution)/shard_map/ppermute | solution.py:41
  9.6 8.3 %collective-permute-start.2 = (f32[4,128,1]{2,1,0:T(8,128)S(1)}, f32[4,128,1]{2,1,0:T(8,128)S(1)}, u32[]{:S(2)}, u32[]{:S(2)}) collective-permute-start(f32[4,128,1]{2,1,0:T(8,128)S(1)} %slice.175), channel_id=1, source_target_pairs={{0,1},{1,2},{2,3},{4,5},{5,6},{6,7},{8,9},{9,10},{10,11},{12,13},{... | collective-permute-start | bytes 6152 | tf_op jit(solution)/shard_map/ppermute | solution.py:41
  13.2 46.7 %copy-start.6 = (f32[3,128,1024]{2,1,0:T(8,128)}, f32[3,128,1024]{2,1,0:T(8,128)S(1)}, u32[]{:S(2)}) copy-start(f32[3,128,1024]{2,1,0:T(8,128)S(1)} %slice.206) | copy-start | bytes 4718596
  20.2 2.9 %collective-permute-start.3 = (f32[128,1024]{1,0:T(8,128)S(1)}, f32[128,1024]{1,0:T(8,128)S(1)}, u32[]{:S(2)}, u32[]{:S(2)}) collective-permute-start(f32[128,1024]{1,0:T(8,128)S(1)} %fusion.30), channel_id=1, source_target_pairs={{0,64},{1,65},{2,66},{3,67},{4,68},{5,69},{6,70},{7,71},{8,72},{9,... | collective-permute-start | bytes 1572872 | tf_op jit(solution)/shard_map/ppermute | solution.py:41
  24.1 3.8 %collective-permute-start.4 = (f32[128,1024]{1,0:T(8,128)S(1)}, f32[128,1024]{1,0:T(8,128)S(1)}, u32[]{:S(2)}, u32[]{:S(2)}) collective-permute-start(f32[128,1024]{1,0:T(8,128)S(1)} %get-tuple-element.40), channel_id=1, source_target_pairs={{0,64},{1,65},{2,66},{3,67},{4,68},{5,69},{6,70},{7,71},{8,72},{9,... | collective-permute-start | bytes 1572872 | tf_op jit(solution)/shard_map/ppermute | solution.py:41
  28.9 3.8 %collective-permute-start.5 = (f32[128,1024]{1,0:T(8,128)S(1)}, f32[128,1024]{1,0:T(8,128)S(1)}, u32[]{:S(2)}, u32[]{:S(2)}) collective-permute-start(f32[128,1024]{1,0:T(8,128)S(1)} %get-tuple-element.36), channel_id=1, source_target_pairs={{64,0},{65,1},{66,2},{67,3},{68,4},{69,5},{70,6},{71,7},{72,8},{73... | collective-permute-start | bytes 1572872 | tf_op jit(solution)/shard_map/ppermute | solution.py:41
  33.0 3.6 %collective-permute-start.6 = (f32[1,128,1024]{2,1,0:T(8,128)S(1)}, f32[1,128,1024]{2,1,0:T(8,128)S(1)}, u32[]{:S(2)}, u32[]{:S(2)}) collective-permute-start(f32[1,128,1024]{2,1,0:T(8,128)S(1)} %bitcast.233), channel_id=1, source_target_pairs={{0,64},{1,65},{2,66},{3,67},{4,68},{5,69},{6,70},{7,71},{8,72},{9,... | collective-permute-start | bytes 1572872 | tf_op jit(solution)/shard_map/ppermute | solution.py:20
  37.4 22.6 %copy-start.13 = (f32[128,1024]{1,0:T(8,128)}, f32[128,1024]{1,0:T(8,128)S(1)}, u32[]{:S(2)}) copy-start(f32[128,1024]{1,0:T(8,128)S(1)} %get-tuple-element.34) | copy-start | bytes 1572868
  37.4 22.6 %copy-start.14 = (f32[128,1024]{1,0:T(8,128)}, f32[128,1024]{1,0:T(8,128)S(1)}, u32[]{:S(2)}) copy-start(f32[128,1024]{1,0:T(8,128)S(1)} %get-tuple-element.35) | copy-start | bytes 1572868
  37.4 22.6 %copy-start.23 = (f32[1,128,1024]{2,1,0:T(8,128)}, f32[1,128,1024]{2,1,0:T(8,128)S(1)}, u32[]{:S(2)}) copy-start(f32[1,128,1024]{2,1,0:T(8,128)S(1)} %get-tuple-element.33) | copy-start | bytes 1572868
  37.4 16.4 %collective-permute-start.7 = (f32[1,128,1024]{2,1,0:T(8,128)S(1)}, f32[1,128,1024]{2,1,0:T(8,128)S(1)}, u32[]{:S(2)}, u32[]{:S(2)}) collective-permute-start(f32[1,128,1024]{2,1,0:T(8,128)S(1)} %get-tuple-element.33), channel_id=1, source_target_pairs={{64,0},{65,1},{66,2},{67,3},{68,4},{69,5},{70,6},{71,7},{72,8},{73... | collective-permute-start | bytes 1572872 | tf_op jit(solution)/shard_map/ppermute | solution.py:21
  39.1 14.6 %collective-permute-start.9 = (f32[4,1,1024]{2,1,0:T(1,128)S(1)}, f32[4,1,1024]{2,1,0:T(1,128)S(1)}, u32[]{:S(2)}, u32[]{:S(2)}) collective-permute-start(f32[4,1,1024]{2,1,0:T(1,128)S(1)} %get-tuple-element.54), channel_id=1, source_target_pairs={{0,4},{4,8},{8,12},{12,16},{16,20},{20,24},{24,28},{28,32},{32,36}... | collective-permute-start | bytes 49160 | tf_op jit(solution)/shard_map/ppermute | solution.py:20
  43.0 10.7 %collective-permute-start.8 = (f32[4,1,1024]{2,1,0:T(1,128)S(1)}, f32[4,1,1024]{2,1,0:T(1,128)S(1)}, u32[]{:S(2)}, u32[]{:S(2)}) collective-permute-start(f32[4,1,1024]{2,1,0:T(1,128)S(1)} %get-tuple-element.55), channel_id=1, source_target_pairs={{4,0},{8,4},{12,8},{16,12},{20,16},{24,20},{28,24},{32,28},{36,32}... | collective-permute-start | bytes 49160 | tf_op jit(solution)/shard_map/ppermute | solution.py:21
  47.3 11.4 %collective-permute-start.10 = (f32[4,128,1]{2,1,0:T(8,128)S(1)}, f32[4,128,1]{2,1,0:T(8,128)S(1)}, u32[]{:S(2)}, u32[]{:S(2)}) collective-permute-start(f32[4,128,1]{2,1,0:T(8,128)S(1)} %get-tuple-element.52), channel_id=1, source_target_pairs={{1,0},{2,1},{3,2},{5,4},{6,5},{7,6},{9,8},{10,9},{11,10},{13,12},{... | collective-permute-start | bytes 6152 | tf_op jit(solution)/shard_map/ppermute | solution.py:21
  48.6 11.3 %collective-permute-start.11 = (f32[4,128,1]{2,1,0:T(8,128)S(1)}, f32[4,128,1]{2,1,0:T(8,128)S(1)}, u32[]{:S(2)}, u32[]{:S(2)}) collective-permute-start(f32[4,128,1]{2,1,0:T(8,128)S(1)} %get-tuple-element.53), channel_id=1, source_target_pairs={{0,1},{1,2},{2,3},{4,5},{5,6},{6,7},{8,9},{9,10},{10,11},{12,13},{... | collective-permute-start | bytes 6152 | tf_op jit(solution)/shard_map/ppermute | solution.py:20
  108.1 38.8 %copy-start.4 = (f32[4,128,1024]{2,1,0:T(8,128)}, f32[4,128,1024]{2,1,0:T(8,128)S(1)}, u32[]{:S(2)}) copy-start(f32[4,128,1024]{2,1,0:T(8,128)S(1)} %multiply_subtract_fusion.1) | copy-start | bytes 6291460
  108.8 2.9 %collective-permute-start.12 = (f32[128,1024]{1,0:T(8,128)S(1)}, f32[128,1024]{1,0:T(8,128)S(1)}, u32[]{:S(2)}, u32[]{:S(2)}) collective-permute-start(f32[128,1024]{1,0:T(8,128)S(1)} %add_multiply_fusion.3), channel_id=1, source_target_pairs={{0,64},{1,65},{2,66},{3,67},{4,68},{5,69},{6,70},{7,71},{8,72},{9,... | collective-permute-start | bytes 1572872 | tf_op jit(solution)/shard_map/ppermute | solution.py:41
  112.8 3.8 %collective-permute-start.13 = (f32[128,1024]{1,0:T(8,128)S(1)}, f32[128,1024]{1,0:T(8,128)S(1)}, u32[]{:S(2)}, u32[]{:S(2)}) collective-permute-start(f32[128,1024]{1,0:T(8,128)S(1)} %get-tuple-element.27), channel_id=1, source_target_pairs={{64,0},{65,1},{66,2},{67,3},{68,4},{69,5},{70,6},{71,7},{72,8},{73... | collective-permute-start | bytes 1572872 | tf_op jit(solution)/shard_map/ppermute | solution.py:41
  116.9 30.1 %copy-start.10 = (f32[128,1024]{1,0:T(8,128)}, f32[128,1024]{1,0:T(8,128)S(1)}, u32[]{:S(2)}) copy-start(f32[128,1024]{1,0:T(8,128)S(1)} %multiply_add_fusion.3) | copy-start | bytes 1572868
  116.9 3.6 %collective-permute-start.14 = (f32[1,128,1024]{2,1,0:T(8,128)S(1)}, f32[1,128,1024]{2,1,0:T(8,128)S(1)}, u32[]{:S(2)}, u32[]{:S(2)}) collective-permute-start(f32[1,128,1024]{2,1,0:T(8,128)S(1)} %bitcast.237), channel_id=1, source_target_pairs={{0,64},{1,65},{2,66},{3,67},{4,68},{5,69},{6,70},{7,71},{8,72},{9,... | collective-permute-start | bytes 1572872 | tf_op jit(solution)/shard_map/ppermute | solution.py:20
  122.6 24.4 %copy-start.15 = (f32[128,1024]{1,0:T(8,128)}, f32[128,1024]{1,0:T(8,128)S(1)}, u32[]{:S(2)}) copy-start(f32[128,1024]{1,0:T(8,128)S(1)} %get-tuple-element.25) | copy-start | bytes 1572868
  122.6 24.4 %copy-start.16 = (f32[128,1024]{1,0:T(8,128)}, f32[128,1024]{1,0:T(8,128)S(1)}, u32[]{:S(2)}) copy-start(f32[128,1024]{1,0:T(8,128)S(1)} %get-tuple-element.26) | copy-start | bytes 1572868
  122.6 24.4 %copy-start.24 = (f32[1,128,1024]{2,1,0:T(8,128)}, f32[1,128,1024]{2,1,0:T(8,128)S(1)}, u32[]{:S(2)}) copy-start(f32[1,128,1024]{2,1,0:T(8,128)S(1)} %get-tuple-element.24) | copy-start | bytes 1572868
  122.6 18.4 %collective-permute-start.15 = (f32[1,128,1024]{2,1,0:T(8,128)S(1)}, f32[1,128,1024]{2,1,0:T(8,128)S(1)}, u32[]{:S(2)}, u32[]{:S(2)}) collective-permute-start(f32[1,128,1024]{2,1,0:T(8,128)S(1)} %get-tuple-element.24), channel_id=1, source_target_pairs={{64,0},{65,1},{66,2},{67,3},{68,4},{69,5},{70,6},{71,7},{72,8},{73... | collective-permute-start | bytes 1572872 | tf_op jit(solution)/shard_map/ppermute | solution.py:21
  124.7 22.3 %copy-start.9 = (f32[4,128,1024]{2,1,0:T(8,128)S(1)}, f32[4,128,1024]{2,1,0:T(8,128)}, u32[]{:S(2)}) copy-start(f32[4,128,1024]{2,1,0:T(8,128)} %param.11) | copy-start | bytes 6291460
  125.5 21.4 %copy-start.3 = (f32[4,128,1024]{2,1,0:T(8,128)S(1)}, f32[4,128,1024]{2,1,0:T(8,128)}, u32[]{:S(2)}) copy-start(f32[4,128,1024]{2,1,0:T(8,128)} %param.7) | copy-start | bytes 6291460
  125.5 21.4 %copy-start.7 = (f32[3,128,1024]{2,1,0:T(8,128)S(1)}, f32[3,128,1024]{2,1,0:T(8,128)}, u32[]{:S(2)}) copy-start(f32[3,128,1024]{2,1,0:T(8,128)} %copy-done.6) | copy-start | bytes 4718596
  125.8 15.1 %collective-permute-start.17 = (f32[4,1,1024]{2,1,0:T(1,128)S(1)}, f32[4,1,1024]{2,1,0:T(1,128)S(1)}, u32[]{:S(2)}, u32[]{:S(2)}) collective-permute-start(f32[4,1,1024]{2,1,0:T(1,128)S(1)} %get-tuple-element.50), channel_id=1, source_target_pairs={{0,4},{4,8},{8,12},{12,16},{16,20},{20,24},{24,28},{28,32},{32,36}... | collective-permute-start | bytes 49160 | tf_op jit(solution)/shard_map/ppermute | solution.py:20
  129.7 11.2 %collective-permute-start.16 = (f32[4,1,1024]{2,1,0:T(1,128)S(1)}, f32[4,1,1024]{2,1,0:T(1,128)S(1)}, u32[]{:S(2)}, u32[]{:S(2)}) collective-permute-start(f32[4,1,1024]{2,1,0:T(1,128)S(1)} %get-tuple-element.51), channel_id=1, source_target_pairs={{4,0},{8,4},{12,8},{16,12},{20,16},{24,20},{28,24},{32,28},{36,32}... | collective-permute-start | bytes 49160 | tf_op jit(solution)/shard_map/ppermute | solution.py:21
  135.1 10.7 %collective-permute-start.18 = (f32[4,128,1]{2,1,0:T(8,128)S(1)}, f32[4,128,1]{2,1,0:T(8,128)S(1)}, u32[]{:S(2)}, u32[]{:S(2)}) collective-permute-start(f32[4,128,1]{2,1,0:T(8,128)S(1)} %get-tuple-element.48), channel_id=1, source_target_pairs={{1,0},{2,1},{3,2},{5,4},{6,5},{7,6},{9,8},{10,9},{11,10},{13,12},{... | collective-permute-start | bytes 6152 | tf_op jit(solution)/shard_map/ppermute | solution.py:21
  136.4 10.6 %collective-permute-start.19 = (f32[4,128,1]{2,1,0:T(8,128)S(1)}, f32[4,128,1]{2,1,0:T(8,128)S(1)}, u32[]{:S(2)}, u32[]{:S(2)}) collective-permute-start(f32[4,128,1]{2,1,0:T(8,128)S(1)} %get-tuple-element.49), channel_id=1, source_target_pairs={{0,1},{1,2},{2,3},{4,5},{5,6},{6,7},{8,9},{9,10},{10,11},{12,13},{... | collective-permute-start | bytes 6152 | tf_op jit(solution)/shard_map/ppermute | solution.py:20
  (22 other events, 158.5 us)
where the time goes:
time: 201 us
  blocking collectives  66.7 us (33%)
  starting transfers between devices  52.4 us (26%)
  other arithmetic  40.2 us (20%)
  waiting for transfers between devices  27.4 us (14%)
  between operations  7.53 us (4%)
  local copies, waits for them, and re-layouts  6.31 us (3%)
    psum x8, blocking collectives, by_axis(): value = lax.psum(value, axis)  66.7 us
    ppermute x6, starting transfers between devices, extended(): lax.ppermute(last, axis, up)  21.6 us
    reduce_sum x2, other arithmetic, paired_sums(): jnp.sum(image * precond)  20 us
    ppermute x8, starting transfers between devices, from_behind(): return lax.ppermute(value, axis, pairs)  17.2 us
    ppermute x8, waiting for transfers between devices, from_behind(): return lax.ppermute(value, axis, pairs)  13.9 us
    ppermute x6, starting transfers between devices, extended(): lax.ppermute(initial, axis, [(b, a) for a, b in up])  13.6 us
    sub x2, other arithmetic, shards(): residual = residual - alpha * along  8.84 us
    ppermute x6, waiting for transfers between devices, extended(): lax.ppermute(initial, axis, [(b, a) for a, b in up])  8.16 us
  transfers between devices with their start and end apart: 20, of which 12 were waited for; matrix products, arithmetic and copies ran while one was open for 2% of the time, Pallas kernels for 0%

commit v1 on v0

--- a/solution.py
+++ b/solution.py
@@ -31,7 +31,7 @@
 
 def by_axis(value, axes):
     for axis in axes:
-        value = lax.psum(value, axis)
+        value = jnp.sum(lax.all_gather(value, axis), axis=0)
     return value
 
 

time: 201 us -> 231 us (1.15)
  local copies, waits for them, and re-layouts: 6.31 us -> 26.9 us
  other arithmetic: 40.2 us -> 51.1 us
  starting transfers between devices: 52.4 us -> 49.4 us
    psum x8 -> x0, blocking collectives: 66.7 us -> none  [by_axis(): value = lax.psum(value, axis)]
    unnamed x0 -> x8, blocking collectives: none -> 66 us
    unnamed x76 -> x126, local copies, waits for them, and re-layouts: 4.74 us -> 26.1 us
    reduce_sum x0 -> x16, other arithmetic: none -> 10.6 us  [by_axis(): value = jnp.sum(lax.all_gather(value, axis), axis=0)]
  transfers between devices with their start and end apart: 20 -> 20, of which waited for: 12 -> 12; matrix products, arithmetic and copies ran while one was open for 2% -> 1% of each run, Pallas kernels for 0% -> 0%
where the time goes in v1:
time: 231 us; the launch traced here: 229 us
  blocking collectives  66 us (29%)
  other arithmetic  51.1 us (22%)
  starting transfers between devices  49.4 us (21%)
  waiting for transfers between devices  28.1 us (12%)
  local copies, waits for them, and re-layouts  26.9 us (12%)
  between operations  7.49 us (3%)
    unnamed x8, blocking collectives  66 us
    unnamed x126, local copies, waits for them, and re-layouts  26.1 us
    ppermute x6, starting transfers between devices, extended(): lax.ppermute(last, axis, up)  19.9 us
    reduce_sum x2, other arithmetic, paired_sums(): jnp.sum(image * precond)  18.3 us
    ppermute x8, starting transfers between devices, from_behind(): return lax.ppermute(value, axis, pairs)  17.2 us
    ppermute x8, waiting for transfers between devices, from_behind(): return lax.ppermute(value, axis, pairs)  14.1 us
    ppermute x6, starting transfers between devices, extended(): lax.ppermute(initial, axis, [(b, a) for a, b in up])  12.4 us
    reduce_sum x16, other arithmetic, by_axis(): value = jnp.sum(lax.all_gather(value, axis), axis=0)  10.6 us
  transfers between devices with their start and end apart: 20, of which 12 were waited for; matrix products, arithmetic and copies ran while one was open for 1% of the time, Pallas kernels for 0%

profile of v1, /device:TPU:2, one launch (start us, length us, event | category | flops | bytes accessed | tf_op | source)
XLA Modules:
  0.0 229.0 jit_solution(15398812846438519659)
XLA Ops:
  0.7 3.1 %multiply_multiply_fusion = f32[4,128,1024]{2,1,0:T(8,128)S(1)} fusion(f32[4,128,1024]{2,1,0:T(8,128)} %param.9, s32[4,128,1024]{2,1,0:T(8,128)} %param.10, f32[4]{0:T(128)S(1)} %compare_convert_fusion), kind=kLoop, calls=%fused_computation.59 | loop fusion | flops 1572864 | bytes 6291472 | tf_op jit(solution)/shard_map/mul | solution.py:102
  3.8 1.9 collective-permute-start
  5.8 3.8 %collective-permute-start.1 = (f32[4,1,1024]{2,1,0:T(1,128)S(1)}, f32[4,1,1024]{2,1,0:T(1,128)S(1)}, u32[]{:S(2)}, u32[]{:S(2)}) collective-permute-start(f32[4,1,1024]{2,1,0:T(1,128)S(1)} %slice.173), channel_id=1, source_target_pairs={{0,4},{4,8},{8,12},{12,16},{16,20},{20,24},{24,28},{28,32},{32,36}... | collective-permute-start | bytes 49160 | tf_op jit(solution)/shard_map/ppermute | solution.py:41
  9.7 3.5 %collective-permute-start.2 = (f32[4,128,1]{2,1,0:T(8,128)S(1)}, f32[4,128,1]{2,1,0:T(8,128)S(1)}, u32[]{:S(2)}, u32[]{:S(2)}) collective-permute-start(f32[4,128,1]{2,1,0:T(8,128)S(1)} %slice.175), channel_id=1, source_target_pairs={{0,1},{1,2},{2,3},{4,5},{5,6},{6,7},{8,9},{9,10},{10,11},{12,13},{... | collective-permute-start | bytes 6152 | tf_op jit(solution)/shard_map/ppermute | solution.py:41
  13.4 4.7 %collective-permute-done.2 = f32[4,128,1]{2,1,0:T(8,128)S(1)} collective-permute-done((f32[4,128,1]{2,1,0:T(8,128)S(1)}, f32[4,128,1]{2,1,0:T(8,128)S(1)}, u32[]{:S(2)}, u32[]{:S(2)}) %collective-permute-start.2) | collective-permute-done | bytes 2080 | tf_op jit(solution)/shard_map/ppermute | solution.py:41
  24.1 2.3 %collective-permute-start.4 = (f32[128,1024]{1,0:T(8,128)S(1)}, f32[128,1024]{1,0:T(8,128)S(1)}, u32[]{:S(2)}, u32[]{:S(2)}) collective-permute-start(f32[128,1024]{1,0:T(8,128)S(1)} %get-tuple-element.40), channel_id=1, source_target_pairs={{0,64},{1,65},{2,66},{3,67},{4,68},{5,69},{6,70},{7,71},{8,72},{9,... | collective-permute-start | bytes 1572872 | tf_op jit(solution)/shard_map/ppermute | solution.py:41
  27.9 2.0 multiply_add_fusion.8
  31.4 2.5 %collective-permute-done.5 = f32[128,1024]{1,0:T(8,128)S(1)} collective-permute-done((f32[128,1024]{1,0:T(8,128)S(1)}, f32[128,1024]{1,0:T(8,128)S(1)}, u32[]{:S(2)}, u32[]{:S(2)}) %collective-permute-start.5) | collective-permute-done | bytes 524320 | tf_op jit(solution)/shard_map/ppermute | solution.py:41
  34.2 2.9 %collective-permute-start.6 = (f32[1,128,1024]{2,1,0:T(8,128)S(1)}, f32[1,128,1024]{2,1,0:T(8,128)}, u32[]{:S(2)}, u32[]{:S(2)}) collective-permute-start(f32[1,128,1024]{2,1,0:T(8,128)S(1)} %bitcast.253), channel_id=1, source_target_pairs={{0,64},{1,65},{2,66},{3,67},{4,68},{5,69},{6,70},{7,71},{8,72},{9,... | collective-permute-start | bytes 1572872 | tf_op jit(solution)/shard_map/ppermute | solution.py:20
  39.0 2.3 %constant_dynamic-update-slice_fusion.4 = (f32[6,128,1024]{2,1,0:T(8,128)S(1)}, f32[1,128,1024]{2,1,0:T(8,128)S(1)}, f32[128,1024]{1,0:T(8,128)S(1)}, f32[128,1024]{1,0:T(8,128)S(1)}) fusion(f32[6,128,1024]{2,1,0:T(8,128)S(1)} %constant_dynamic-update-slice_fusion.5, f32[128,1024]{1,0:T(8,128)} %get-tuple-element.39, f32[128,1024]{1,0:T(8,128)} %copy-done.26, ...), kind=kLoop, calls=%fused_computation.133 | loop fusion | flops 786432 | bytes 5767168
  43.0 4.6 %collective-permute-start.8 = (f32[4,1,1024]{2,1,0:T(1,128)S(1)}, f32[4,1,1024]{2,1,0:T(1,128)S(1)}, u32[]{:S(2)}, u32[]{:S(2)}) collective-permute-start(f32[4,1,1024]{2,1,0:T(1,128)S(1)} %get-tuple-element.55), channel_id=1, source_target_pairs={{4,0},{8,4},{12,8},{16,12},{20,16},{24,20},{28,24},{32,28},{36,32}... | collective-permute-start | bytes 49160 | tf_op jit(solution)/shard_map/ppermute | solution.py:21
  47.6 1.9 collective-permute-start.9
  51.0 5.0 %collective-permute-start.11 = (f32[4,128,1]{2,1,0:T(8,128)S(1)}, f32[4,128,1]{2,1,0:T(8,128)S(1)}, u32[]{:S(2)}, u32[]{:S(2)}) collective-permute-start(f32[4,128,1]{2,1,0:T(8,128)S(1)} %get-tuple-element.53), channel_id=1, source_target_pairs={{0,1},{1,2},{2,3},{4,5},{5,6},{6,7},{8,9},{9,10},{10,11},{12,13},{... | collective-permute-start | bytes 6152 | tf_op jit(solution)/shard_map/ppermute | solution.py:20
  56.2 4.8 %collective-permute-done.10 = f32[4,128,1]{2,1,0:T(8,128)S(1)} collective-permute-done((f32[4,128,1]{2,1,0:T(8,128)S(1)}, f32[4,128,1]{2,1,0:T(8,128)S(1)}, u32[]{:S(2)}, u32[]{:S(2)}) %collective-permute-start.10) | collective-permute-done | bytes 2080 | tf_op jit(solution)/shard_map/ppermute | solution.py:21
  62.6 9.8 %multiply_reduce_fusion.2 = (f32[]{:T(128)}, f32[]{:T(128)}, f32[4,128,1024]{2,1,0:T(8,128)}) fusion(f32[1,128,1024]{2,1,0:T(8,128)S(1)} %bitcast.255, f32[1,128,1024]{2,1,0:T(8,128)S(1)} %bitcast.265, f32[1,128,1024]{2,1,0:T(8,128)S(1)} %bitcast.262, f32[1,128,1024]{2,1,0:T(8,128)S(1)} %get-tuple-element.33, f32[4,128,1024]{2,1,0:T(8,128)S(1)} %copy-done.8, ...), kind=kLoop, calls=%fused_computation.56 | loop fusion | flops 25690112 | bytes 25219080 | tf_op jit(solution)/shard_map/reduce_sum | solution.py:92
  75.9 2.4 %all-reduce.31 = (f32[2]{0:T(128)S(1)}, f32[2]{0:T(128)S(1)}) all-reduce(f32[2]{0:T(128)S(1)} %dynamic-update-slice, f32[2]{0:T(128)S(1)} %dynamic-update-slice.4), channel_id=1, replica_groups=mesh['layer'=2,'px_0'=4,'px_1'=4,'py'=4] {'layer'}, use_global_device_ids=true, to_apply=%add.8 | all-reduce | flops 4 | bytes 32
  82.9 8.6 %all-reduce.29 = (f32[4]{0:T(128)S(1)}, f32[4]{0:T(128)S(1)}) all-reduce(f32[4]{0:T(128)S(1)} %dynamic-update-slice.1, f32[4]{0:T(128)S(1)} %dynamic-update-slice.5), channel_id=1, replica_groups=mesh['layer'=2,'px_0'=4,'px_1'=4,'py'=4] {'px_0'}, use_global_device_ids=true, to_apply=%add.9 | all-reduce | flops 8 | bytes 64
  96.2 11.6 %all-reduce.27 = (f32[4]{0:T(128)S(1)}, f32[4]{0:T(128)S(1)}) all-reduce(f32[4]{0:T(128)S(1)} %dynamic-update-slice.2, f32[4]{0:T(128)S(1)} %dynamic-update-slice.6), channel_id=1, replica_groups=mesh['layer'=2,'px_0'=4,'px_1'=4,'py'=4] {'px_1'}, use_global_device_ids=true, to_apply=%add.10 | all-reduce | flops 8 | bytes 64
  111.7 12.3 %all-reduce.25 = (f32[4]{0:T(128)S(1)}, f32[4]{0:T(128)S(1)}) all-reduce(f32[4]{0:T(128)S(1)} %dynamic-update-slice.3, f32[4]{0:T(128)S(1)} %dynamic-update-slice.7), channel_id=1, replica_groups=mesh['layer'=2,'px_0'=4,'px_1'=4,'py'=4] {'py'}, use_global_device_ids=true, to_apply=%add.11 | all-reduce | flops 8 | bytes 64
  126.7 2.8 %multiply_subtract_fusion.1 = f32[4,128,1024]{2,1,0:T(8,128)S(1)} fusion(f32[4,128,1024]{2,1,0:T(8,128)} %param.6, f32[4,128,1024]{2,1,0:T(8,128)} %get-tuple-element.31, f32[]{:T(128)S(6)} %div.44), kind=kLoop, calls=%fused_computation.55 | loop fusion | flops 1048576 | bytes 6291460 | tf_op jit(solution)/shard_map/sub | solution.py:152
  135.5 2.5 %collective-permute-done.13 = f32[128,1024]{1,0:T(8,128)S(1)} collective-permute-done((f32[128,1024]{1,0:T(8,128)S(1)}, f32[128,1024]{1,0:T(8,128)S(1)}, u32[]{:S(2)}, u32[]{:S(2)}) %collective-permute-start.13) | collective-permute-done | bytes 524320 | tf_op jit(solution)/shard_map/ppermute | solution.py:41
  138.3 2.1 collective-permute-start.14
  144.1 2.6 %collective-permute-start.16 = (f32[4,1,1024]{2,1,0:T(1,128)S(1)}, f32[4,1,1024]{2,1,0:T(1,128)S(1)}, u32[]{:S(2)}, u32[]{:S(2)}) collective-permute-start(f32[4,1,1024]{2,1,0:T(1,128)S(1)} %get-tuple-element.51), channel_id=1, source_target_pairs={{4,0},{8,4},{12,8},{16,12},{20,16},{24,20},{28,24},{32,28},{36,32}... | collective-permute-start | bytes 49160 | tf_op jit(solution)/shard_map/ppermute | solution.py:21
  146.8 3.5 %collective-permute-start.17 = (f32[4,1,1024]{2,1,0:T(1,128)S(1)}, f32[4,1,1024]{2,1,0:T(1,128)S(1)}, u32[]{:S(2)}, u32[]{:S(2)}) collective-permute-start(f32[4,1,1024]{2,1,0:T(1,128)S(1)} %get-tuple-element.50), channel_id=1, source_target_pairs={{0,4},{4,8},{8,12},{12,16},{16,20},{20,24},{24,28},{28,32},{32,36}... | collective-permute-start | bytes 49160 | tf_op jit(solution)/shard_map/ppermute | solution.py:20
  151.8 4.6 %collective-permute-start.19 = (f32[4,128,1]{2,1,0:T(8,128)S(1)}, f32[4,128,1]{2,1,0:T(8,128)S(1)}, u32[]{:S(2)}, u32[]{:S(2)}) collective-permute-start(f32[4,128,1]{2,1,0:T(8,128)S(1)} %get-tuple-element.49), channel_id=1, source_target_pairs={{0,1},{1,2},{2,3},{4,5},{5,6},{6,7},{8,9},{9,10},{10,11},{12,13},{... | collective-permute-start | bytes 6152 | tf_op jit(solution)/shard_map/ppermute | solution.py:20
  156.5 4.7 %collective-permute-done.18 = f32[4,128,1]{2,1,0:T(8,128)S(1)} collective-permute-done((f32[4,128,1]{2,1,0:T(8,128)S(1)}, f32[4,128,1]{2,1,0:T(8,128)S(1)}, u32[]{:S(2)}, u32[]{:S(2)}) %collective-permute-start.18) | collective-permute-done | bytes 2080 | tf_op jit(solution)/shard_map/ppermute | solution.py:21
  162.4 8.5 %multiply_reduce_fusion = (f32[]{:T(128)}, f32[]{:T(128)}, f32[4,128,1024]{2,1,0:T(8,128)}) fusion(f32[1,128,1024]{2,1,0:T(8,128)S(1)} %bitcast.259, f32[1,128,1024]{2,1,0:T(8,128)S(1)} %bitcast.271, f32[1,128,1024]{2,1,0:T(8,128)S(1)} %bitcast.268, f32[1,128,1024]{2,1,0:T(8,128)S(1)} %get-tuple-element.24, f32[4,128,1024]{2,1,0:T(8,128)S(1)} %multiply_subtract_fusion.1, ...), kind=kLoop, calls=%fused_computation.53 | loop fusion | flops 25690112 | bytes 25219080 | tf_op jit(solution)/shard_map/reduce_sum | solution.py:92
  173.8 2.4 %all-reduce.30 = (f32[2]{0:T(128)S(1)}, f32[2]{0:T(128)S(1)}) all-reduce(f32[2]{0:T(128)S(1)} %dynamic-update-slice.8, f32[2]{0:T(128)S(1)} %dynamic-update-slice.12), channel_id=1, replica_groups=mesh['layer'=2,'px_0'=4,'px_1'=4,'py'=4] {'layer'}, use_global_device_ids=true, to_apply=%add.16 | all-reduce | flops 4 | bytes 32
  180.3 8.8 %all-reduce.28 = (f32[4]{0:T(128)S(1)}, f32[4]{0:T(128)S(1)}) all-reduce(f32[4]{0:T(128)S(1)} %dynamic-update-slice.9, f32[4]{0:T(128)S(1)} %dynamic-update-slice.13), channel_id=1, replica_groups=mesh['layer'=2,'px_0'=4,'px_1'=4,'py'=4] {'px_0'}, use_global_device_ids=true, to_apply=%add.17 | all-reduce | flops 8 | bytes 64
  193.3 9.7 %all-reduce.26 = (f32[4]{0:T(128)S(1)}, f32[4]{0:T(128)S(1)}) all-reduce(f32[4]{0:T(128)S(1)} %dynamic-update-slice.10, f32[4]{0:T(128)S(1)} %dynamic-update-slice.14), channel_id=1, replica_groups=mesh['layer'=2,'px_0'=4,'px_1'=4,'py'=4] {'px_1'}, use_global_device_ids=true, to_apply=%add.18 | all-reduce | flops 8 | bytes 64
  207.1 10.2 %all-reduce.24 = (f32[4]{0:T(128)S(1)}, f32[4]{0:T(128)S(1)}) all-reduce(f32[4]{0:T(128)S(1)} %dynamic-update-slice.11, f32[4]{0:T(128)S(1)} %dynamic-update-slice.15), channel_id=1, replica_groups=mesh['layer'=2,'px_0'=4,'px_1'=4,'py'=4] {'py'}, use_global_device_ids=true, to_apply=%add.19 | all-reduce | flops 8 | bytes 64
  223.0 6.0 %multiply_subtract_fusion = (f32[4,128,1024]{2,1,0:T(8,128)}, f32[4,128,1024]{2,1,0:T(8,128)}) fusion(f32[4,128,1024]{2,1,0:T(8,128)} %copy-done.6, f32[4,128,1024]{2,1,0:T(8,128)} %get-tuple-element.22, f32[4,128,1024]{2,1,0:T(8,128)} %get-tuple-element.31, f32[]{:T(128)S(6)} %div.45, f32[]{:T(128)S(6)} %div.47, f32[1,128,1024]{2,1,0:T(8,128)} %bitcast.260, ...), kind=kLoop, calls=%fused_computation.51 | loop fusion | flops 7864320 | bytes 14680076 | tf_op jit(solution)/shard_map/sub | solution.py:152
  (190 shorter events, 63.2 us)
Async XLA Ops:
  3.8 14.2 %collective-permute-start = (f32[1,128,1024]{2,1,0:T(8,128)S(1)}, f32[1,128,1024]{2,1,0:T(8,128)S(1)}, u32[]{:S(2)}, u32[]{:S(2)}) collective-permute-start(f32[1,128,1024]{2,1,0:T(8,128)S(1)} %slice.202), channel_id=1, source_target_pairs={{0,64},{1,65},{2,66},{3,67},{4,68},{5,69},{6,70},{7,71},{8,72},{9,... | collective-permute-start | bytes 1572872 | tf_op jit(solution)/shard_map/ppermute | solution.py:41
  5.8 12.3 %collective-permute-start.1 = (f32[4,1,1024]{2,1,0:T(1,128)S(1)}, f32[4,1,1024]{2,1,0:T(1,128)S(1)}, u32[]{:S(2)}, u32[]{:S(2)}) collective-permute-start(f32[4,1,1024]{2,1,0:T(1,128)S(1)} %slice.173), channel_id=1, source_target_pairs={{0,4},{4,8},{8,12},{12,16},{16,20},{20,24},{24,28},{28,32},{32,36}... | collective-permute-start | bytes 49160 | tf_op jit(solution)/shard_map/ppermute | solution.py:41
  9.7 8.3 %collective-permute-start.2 = (f32[4,128,1]{2,1,0:T(8,128)S(1)}, f32[4,128,1]{2,1,0:T(8,128)S(1)}, u32[]{:S(2)}, u32[]{:S(2)}) collective-permute-start(f32[4,128,1]{2,1,0:T(8,128)S(1)} %slice.175), channel_id=1, source_target_pairs={{0,1},{1,2},{2,3},{4,5},{5,6},{6,7},{8,9},{9,10},{10,11},{12,13},{... | collective-permute-start | bytes 6152 | tf_op jit(solution)/shard_map/ppermute | solution.py:41
  20.3 2.9 %collective-permute-start.3 = (f32[128,1024]{1,0:T(8,128)S(1)}, f32[128,1024]{1,0:T(8,128)S(1)}, u32[]{:S(2)}, u32[]{:S(2)}) collective-permute-start(f32[128,1024]{1,0:T(8,128)S(1)} %fusion.30), channel_id=1, source_target_pairs={{0,64},{1,65},{2,66},{3,67},{4,68},{5,69},{6,70},{7,71},{8,72},{9,... | collective-permute-start | bytes 1572872 | tf_op jit(solution)/shard_map/ppermute | solution.py:41
  24.1 3.8 %collective-permute-start.4 = (f32[128,1024]{1,0:T(8,128)S(1)}, f32[128,1024]{1,0:T(8,128)S(1)}, u32[]{:S(2)}, u32[]{:S(2)}) collective-permute-start(f32[128,1024]{1,0:T(8,128)S(1)} %get-tuple-element.40), channel_id=1, source_target_pairs={{0,64},{1,65},{2,66},{3,67},{4,68},{5,69},{6,70},{7,71},{8,72},{9,... | collective-permute-start | bytes 1572872 | tf_op jit(solution)/shard_map/ppermute | solution.py:41
  29.9 3.9 %collective-permute-start.5 = (f32[128,1024]{1,0:T(8,128)S(1)}, f32[128,1024]{1,0:T(8,128)S(1)}, u32[]{:S(2)}, u32[]{:S(2)}) collective-permute-start(f32[128,1024]{1,0:T(8,128)S(1)} %get-tuple-element.36), channel_id=1, source_target_pairs={{64,0},{65,1},{66,2},{67,3},{68,4},{69,5},{70,6},{71,7},{72,8},{73... | collective-permute-start | bytes 1572872 | tf_op jit(solution)/shard_map/ppermute | solution.py:41
  34.2 3.7 %collective-permute-start.6 = (f32[1,128,1024]{2,1,0:T(8,128)S(1)}, f32[1,128,1024]{2,1,0:T(8,128)}, u32[]{:S(2)}, u32[]{:S(2)}) collective-permute-start(f32[1,128,1024]{2,1,0:T(8,128)S(1)} %bitcast.253), channel_id=1, source_target_pairs={{0,64},{1,65},{2,66},{3,67},{4,68},{5,69},{6,70},{7,71},{8,72},{9,... | collective-permute-start | bytes 1572872 | tf_op jit(solution)/shard_map/ppermute | solution.py:20
  39.0 23.6 %copy-start.13 = (f32[4,128,1024]{2,1,0:T(8,128)S(1)}, f32[4,128,1024]{2,1,0:T(8,128)}, u32[]{:S(2)}) copy-start(f32[4,128,1024]{2,1,0:T(8,128)} %param.11) | copy-start | bytes 6291460
  41.3 21.3 %copy-start.18 = (f32[128,1024]{1,0:T(8,128)}, f32[128,1024]{1,0:T(8,128)S(1)}, u32[]{:S(2)}) copy-start(f32[128,1024]{1,0:T(8,128)S(1)} %get-tuple-element.34) | copy-start | bytes 1572868
  41.4 21.2 %copy-start.19 = (f32[128,1024]{1,0:T(8,128)}, f32[128,1024]{1,0:T(8,128)S(1)}, u32[]{:S(2)}) copy-start(f32[128,1024]{1,0:T(8,128)S(1)} %get-tuple-element.35) | copy-start | bytes 1572868
  41.4 21.2 %copy-start.28 = (f32[1,128,1024]{2,1,0:T(8,128)}, f32[1,128,1024]{2,1,0:T(8,128)S(1)}, u32[]{:S(2)}) copy-start(f32[1,128,1024]{2,1,0:T(8,128)S(1)} %get-tuple-element.33) | copy-start | bytes 1572868
  41.4 14.7 %collective-permute-start.7 = (f32[1,128,1024]{2,1,0:T(8,128)S(1)}, f32[1,128,1024]{2,1,0:T(8,128)S(1)}, u32[]{:S(2)}, u32[]{:S(2)}) collective-permute-start(f32[1,128,1024]{2,1,0:T(8,128)S(1)} %get-tuple-element.33), channel_id=1, source_target_pairs={{64,0},{65,1},{66,2},{67,3},{68,4},{69,5},{70,6},{71,7},{72,8},{73... | collective-permute-start | bytes 1572872 | tf_op jit(solution)/shard_map/ppermute | solution.py:21
  42.7 19.9 %copy-start.10 = (f32[3,128,1024]{2,1,0:T(8,128)S(1)}, f32[3,128,1024]{2,1,0:T(8,128)}, u32[]{:S(2)}) copy-start(f32[3,128,1024]{2,1,0:T(8,128)} %copy-done.9) | copy-start | bytes 4718596
  43.0 13.0 %collective-permute-start.8 = (f32[4,1,1024]{2,1,0:T(1,128)S(1)}, f32[4,1,1024]{2,1,0:T(1,128)S(1)}, u32[]{:S(2)}, u32[]{:S(2)}) collective-permute-start(f32[4,1,1024]{2,1,0:T(1,128)S(1)} %get-tuple-element.55), channel_id=1, source_target_pairs={{4,0},{8,4},{12,8},{16,12},{20,16},{24,20},{28,24},{32,28},{36,32}... | collective-permute-start | bytes 49160 | tf_op jit(solution)/shard_map/ppermute | solution.py:21
  47.6 8.5 %collective-permute-start.9 = (f32[4,1,1024]{2,1,0:T(1,128)S(1)}, f32[4,1,1024]{2,1,0:T(1,128)S(1)}, u32[]{:S(2)}, u32[]{:S(2)}) collective-permute-start(f32[4,1,1024]{2,1,0:T(1,128)S(1)} %get-tuple-element.54), channel_id=1, source_target_pairs={{0,4},{4,8},{8,12},{12,16},{16,20},{20,24},{24,28},{28,32},{32,36}... | collective-permute-start | bytes 49160 | tf_op jit(solution)/shard_map/ppermute | solution.py:20
  49.7 11.4 %collective-permute-start.10 = (f32[4,128,1]{2,1,0:T(8,128)S(1)}, f32[4,128,1]{2,1,0:T(8,128)S(1)}, u32[]{:S(2)}, u32[]{:S(2)}) collective-permute-start(f32[4,128,1]{2,1,0:T(8,128)S(1)} %get-tuple-element.52), channel_id=1, source_target_pairs={{1,0},{2,1},{3,2},{5,4},{6,5},{7,6},{9,8},{10,9},{11,10},{13,12},{... | collective-permute-start | bytes 6152 | tf_op jit(solution)/shard_map/ppermute | solution.py:21
  51.0 11.6 %collective-permute-start.11 = (f32[4,128,1]{2,1,0:T(8,128)S(1)}, f32[4,128,1]{2,1,0:T(8,128)S(1)}, u32[]{:S(2)}, u32[]{:S(2)}) collective-permute-start(f32[4,128,1]{2,1,0:T(8,128)S(1)} %get-tuple-element.53), channel_id=1, source_target_pairs={{0,1},{1,2},{2,3},{4,5},{5,6},{6,7},{8,9},{9,10},{10,11},{12,13},{... | collective-permute-start | bytes 6152 | tf_op jit(solution)/shard_map/ppermute | solution.py:20
  56.2 26.1 %copy-start.38 = (u32[128]{0:T(128)S(1)}, u32[128]{0:T(128)}, u32[]{:S(2)}) copy-start(u32[128]{0:T(128)} %constant.45) | copy-start | bytes 1540
  56.2 39.4 %copy-start.37 = (u32[128]{0:T(128)S(1)}, u32[128]{0:T(128)}, u32[]{:S(2)}) copy-start(u32[128]{0:T(128)} %constant.50) | copy-start | bytes 1540
  129.5 32.8 %copy-start.6 = (f32[4,128,1024]{2,1,0:T(8,128)}, f32[4,128,1024]{2,1,0:T(8,128)S(1)}, u32[]{:S(2)}) copy-start(f32[4,128,1024]{2,1,0:T(8,128)S(1)} %multiply_subtract_fusion.1) | copy-start | bytes 6291460
  130.3 2.9 %collective-permute-start.12 = (f32[128,1024]{1,0:T(8,128)S(1)}, f32[128,1024]{1,0:T(8,128)S(1)}, u32[]{:S(2)}, u32[]{:S(2)}) collective-permute-start(f32[128,1024]{1,0:T(8,128)S(1)} %add_multiply_fusion.3), channel_id=1, source_target_pairs={{0,64},{1,65},{2,66},{3,67},{4,68},{5,69},{6,70},{7,71},{8,72},{9,... | collective-permute-start | bytes 1572872 | tf_op jit(solution)/shard_map/ppermute | solution.py:41
  134.2 3.8 %collective-permute-start.13 = (f32[128,1024]{1,0:T(8,128)S(1)}, f32[128,1024]{1,0:T(8,128)S(1)}, u32[]{:S(2)}, u32[]{:S(2)}) collective-permute-start(f32[128,1024]{1,0:T(8,128)S(1)} %get-tuple-element.27), channel_id=1, source_target_pairs={{64,0},{65,1},{66,2},{67,3},{68,4},{69,5},{70,6},{71,7},{72,8},{73... | collective-permute-start | bytes 1572872 | tf_op jit(solution)/shard_map/ppermute | solution.py:41
  138.3 24.0 %copy-start.15 = (f32[128,1024]{1,0:T(8,128)}, f32[128,1024]{1,0:T(8,128)S(1)}, u32[]{:S(2)}) copy-start(f32[128,1024]{1,0:T(8,128)S(1)} %multiply_add_fusion.3) | copy-start | bytes 1572868
  138.3 3.6 %collective-permute-start.14 = (f32[1,128,1024]{2,1,0:T(8,128)S(1)}, f32[1,128,1024]{2,1,0:T(8,128)S(1)}, u32[]{:S(2)}, u32[]{:S(2)}) collective-permute-start(f32[1,128,1024]{2,1,0:T(8,128)S(1)} %bitcast.257), channel_id=1, source_target_pairs={{0,64},{1,65},{2,66},{3,67},{4,68},{5,69},{6,70},{7,71},{8,72},{9,... | collective-permute-start | bytes 1572872 | tf_op jit(solution)/shard_map/ppermute | solution.py:20
  142.5 19.9 %copy-start.20 = (f32[128,1024]{1,0:T(8,128)}, f32[128,1024]{1,0:T(8,128)S(1)}, u32[]{:S(2)}) copy-start(f32[128,1024]{1,0:T(8,128)S(1)} %get-tuple-element.25) | copy-start | bytes 1572868
  142.5 19.9 %copy-start.21 = (f32[128,1024]{1,0:T(8,128)}, f32[128,1024]{1,0:T(8,128)S(1)}, u32[]{:S(2)}) copy-start(f32[128,1024]{1,0:T(8,128)S(1)} %get-tuple-element.26) | copy-start | bytes 1572868
  142.5 19.9 %copy-start.29 = (f32[1,128,1024]{2,1,0:T(8,128)}, f32[1,128,1024]{2,1,0:T(8,128)S(1)}, u32[]{:S(2)}) copy-start(f32[1,128,1024]{2,1,0:T(8,128)S(1)} %get-tuple-element.24) | copy-start | bytes 1572868
  142.5 13.9 %collective-permute-start.15 = (f32[1,128,1024]{2,1,0:T(8,128)S(1)}, f32[1,128,1024]{2,1,0:T(8,128)S(1)}, u32[]{:S(2)}, u32[]{:S(2)}) collective-permute-start(f32[1,128,1024]{2,1,0:T(8,128)S(1)} %get-tuple-element.24), channel_id=1, source_target_pairs={{64,0},{65,1},{66,2},{67,3},{68,4},{69,5},{70,6},{71,7},{72,8},{73... | collective-permute-start | bytes 1572872 | tf_op jit(solution)/shard_map/ppermute | solution.py:21
  144.1 12.2 %collective-permute-start.16 = (f32[4,1,1024]{2,1,0:T(1,128)S(1)}, f32[4,1,1024]{2,1,0:T(1,128)S(1)}, u32[]{:S(2)}, u32[]{:S(2)}) collective-permute-start(f32[4,1,1024]{2,1,0:T(1,128)S(1)} %get-tuple-element.51), channel_id=1, source_target_pairs={{4,0},{8,4},{12,8},{16,12},{20,16},{24,20},{28,24},{32,28},{36,32}... | collective-permute-start | bytes 49160 | tf_op jit(solution)/shard_map/ppermute | solution.py:21
  146.8 9.6 %collective-permute-start.17 = (f32[4,1,1024]{2,1,0:T(1,128)S(1)}, f32[4,1,1024]{2,1,0:T(1,128)S(1)}, u32[]{:S(2)}, u32[]{:S(2)}) collective-permute-start(f32[4,1,1024]{2,1,0:T(1,128)S(1)} %get-tuple-element.50), channel_id=1, source_target_pairs={{0,4},{4,8},{8,12},{12,16},{16,20},{20,24},{24,28},{28,32},{32,36}... | collective-permute-start | bytes 49160 | tf_op jit(solution)/shard_map/ppermute | solution.py:20
  150.5 10.7 %collective-permute-start.18 = (f32[4,128,1]{2,1,0:T(8,128)S(1)}, f32[4,128,1]{2,1,0:T(8,128)S(1)}, u32[]{:S(2)}, u32[]{:S(2)}) collective-permute-start(f32[4,128,1]{2,1,0:T(8,128)S(1)} %get-tuple-element.48), channel_id=1, source_target_pairs={{1,0},{2,1},{3,2},{5,4},{6,5},{7,6},{9,8},{10,9},{11,10},{13,12},{... | collective-permute-start | bytes 6152 | tf_op jit(solution)/shard_map/ppermute | solution.py:21
  151.8 10.6 %collective-permute-start.19 = (f32[4,128,1]{2,1,0:T(8,128)S(1)}, f32[4,128,1]{2,1,0:T(8,128)S(1)}, u32[]{:S(2)}, u32[]{:S(2)}) collective-permute-start(f32[4,128,1]{2,1,0:T(8,128)S(1)} %get-tuple-element.49), channel_id=1, source_target_pairs={{0,1},{1,2},{2,3},{4,5},{5,6},{6,7},{8,9},{9,10},{10,11},{12,13},{... | collective-permute-start | bytes 6152 | tf_op jit(solution)/shard_map/ppermute | solution.py:20
  (29 other events, 269.0 us)
